TPU v7x, 32 devices: a whole 2x2x4 slice. The times are simulated.
32 devices in a mesh: seq: 8 (over z, core), batch: 4 (over y, x).
Axes of the slice: x: 2, y: 2, z: 4, core: 2. Of those that a mesh axis runs over, the one named last changes fastest.
Arguments:
- tokens: bfloat16 [4, 2048, 1152], P('batch', 'seq'), may hold values from -6 to 6
- long_skip: bfloat16 [4, 2048, 1152], P('batch', 'seq'), may hold values from -6 to 6
- lengths: int32 [4, 4], P('batch'), may hold values from 0 to 1026, as said below
- skip_weight: bfloat16 [2304, 1152], replicated, may hold values from -0.125 to 0.125
- skip_bias: bfloat16 [1152], replicated, may hold values from -3 to 3
- attention_gain: bfloat16 [1152], replicated, may hold values from 0.099609375 to 1.8984375
- attention_shift: bfloat16 [1152], replicated, may hold values from -3 to 3
- qkv_weight: bfloat16 [1152, 3456], replicated, may hold values from -0.1875 to 0.1875
- out_weight: bfloat16 [1152, 1152], replicated, may hold values from -2 to 2
- out_bias: bfloat16 [1152], replicated, may hold values from -3 to 3
- mlp_gain: bfloat16 [1152], replicated, may hold values from 0.099609375 to 1.8984375
- mlp_shift: bfloat16 [1152], replicated, may hold values from -3 to 3
- hidden_weight: bfloat16 [1152, 4608], replicated, may hold values from -0.1875 to 0.1875
- hidden_bias: bfloat16 [4608], replicated, may hold values from -3 to 3
- down_weight: bfloat16 [4608, 1152], replicated, may hold values from -0.09375 to 0.09375
- down_bias: bfloat16 [1152], replicated, may hold values from -3 to 3
- cotangent: bfloat16 [4, 2048, 1152], P('batch', 'seq'), may hold values from -6 to 6
Outputs:
- output: bfloat16 [4, 2048, 1152], P('batch', 'seq')
- grad_tokens: float32 [4, 2048, 1152], P('batch', 'seq')
- grad_long_skip: float32 [4, 2048, 1152], P('batch', 'seq')
- grad_skip_weight: float32 [2304, 1152], P('batch', 'seq')
- grad_skip_bias: float32 [1152], replicated
- grad_attention_gain: float32 [1152], replicated
- grad_attention_shift: float32 [1152], replicated
- grad_qkv_weight: float32 [1152, 3456], P('batch', 'seq')
- grad_out_weight: float32 [1152, 1152], P('batch', 'seq')
- grad_out_bias: float32 [1152], replicated
- grad_mlp_gain: float32 [1152], replicated
- grad_mlp_shift: float32 [1152], replicated
- grad_hidden_weight: float32 [1152, 4608], P('batch', 'seq')
- grad_hidden_bias: float32 [4608], replicated
- grad_down_weight: float32 [4608, 1152], P('batch', 'seq')
- grad_down_bias: float32 [1152], replicated
Inputs may be any that keep to these rules, and one draw needn't show every extreme that they name: Row g lists the lengths of group g's items in the order in which they lie along the group's 2048 positions. Each entry is 258, 1026 or 0, every row has one or more entries 1026, zeros stand only after the last nonzero entry, and the row's total leaves fewer than 258 positions of padding at the end.
All inputs are finite; a program needn't handle non-finite values.
Results may differ from a plain program's by a relative error of at most 0.013.
Values may be sent and summed in bfloat16 or wider, within the bound.
A program may use at most 256 MiB of HBM per device.

v0:
```python
import math
import jax
import jax.numpy as jnp
from jax import lax
from jax.sharding import PartitionSpec as P

HD = 72
norm_eps = 1e-05


def product(left, right):
    return jnp.dot(left, right, preferred_element_type=jnp.float32)


def contract_rows(left, right):
    return lax.dot_general(
        left, right, (((0,), (0,)), ((), ())), preferred_element_type=jnp.float32
    )


def times_transposed(left, right):
    return lax.dot_general(
        left, right, (((1,), (1,)), ((), ())), preferred_element_type=jnp.float32
    )


def column_sums(values):
    return jnp.sum(values.astype(jnp.float32), axis=0)


def layer_norm(inputs, gain, shift):
    mean_row = jnp.mean(inputs, axis=-1, keepdims=True)
    centred = inputs - mean_row
    spread = jnp.mean(centred * centred, axis=-1, keepdims=True)
    return centred * lax.rsqrt(spread + norm_eps) * gain + shift


def exact_gelu(inputs):
    return jax.nn.gelu(inputs, approximate=False)


def segments(row_lengths, group_len):
    ends = jnp.cumsum(row_lengths)
    places = jnp.arange(group_len, dtype=jnp.int32)
    return jnp.sum((places[:, None] >= ends[None, :]).astype(jnp.int32), axis=1)


def score_block(query_block, key_heads, seg_block, segment):
    raw = jnp.einsum("bhd,khd->hbk", query_block, key_heads, preferred_element_type=jnp.float32)
    scores = raw * (1.0 / math.sqrt(HD))
    allowed = (seg_block[:, None] == segment[None, :])[None]
    return jnp.where(allowed, scores, -jnp.inf)


def attend_forward(query_heads, key_flat, value_flat, segment):
    length, head_cols = query_heads.shape
    head_count = head_cols // HD
    block_rows = min(512, length)
    block_count = length // block_rows
    key_heads = key_flat.reshape(length, head_count, HD)
    value_heads = value_flat.reshape(length, head_count, HD)

    def one_block(pieces):
        query_block, seg_block = pieces
        scores = score_block(query_block, key_heads, seg_block, segment)
        row_max = jnp.max(scores, axis=2, keepdims=True)
        log_total = row_max + jnp.log(jnp.sum(jnp.exp(scores - row_max), axis=2, keepdims=True))
        probs_low = jnp.exp(scores - log_total).astype(jnp.bfloat16)
        context = jnp.einsum(
            "hbk,khd->bhd", probs_low, value_heads, preferred_element_type=jnp.float32
        )
        return (context.astype(jnp.bfloat16).reshape(block_rows, head_cols), log_total)

    context, log_total = lax.map(
        one_block,
        (
            query_heads.reshape(block_count, block_rows, head_count, HD),
            segment.reshape(block_count, block_rows),
        ),
    )
    return (context.reshape(length, head_cols), log_total)


def attend_backward(query_heads, key_flat, value_flat, segment, grad_context, log_total):
    length, head_cols = query_heads.shape
    head_count = head_cols // HD
    block_rows = min(512, length)
    block_count = length // block_rows
    score_scale = 1.0 / math.sqrt(HD)
    key_heads = key_flat.reshape(length, head_count, HD)
    value_heads = value_flat.reshape(length, head_count, HD)

    def one_block(totals, pieces):
        grad_keys, grad_values = totals
        query_block, seg_block, grad_block, total_block = pieces
        scores = score_block(query_block, key_heads, seg_block, segment)
        prob_full = jnp.exp(scores - total_block)
        probs_low = prob_full.astype(jnp.bfloat16)
        grad_values = grad_values + jnp.einsum(
            "hbk,bhd->khd", probs_low, grad_block, preferred_element_type=jnp.float32
        )
        grad_probs = jnp.einsum(
            "bhd,khd->hbk", grad_block, value_heads, preferred_element_type=jnp.float32
        )
        row_delta = jnp.sum(prob_full * grad_probs, axis=2, keepdims=True)
        grad_scores = (prob_full * (grad_probs - row_delta)).astype(jnp.bfloat16)
        grad_query = (
            jnp.einsum("hbk,khd->bhd", grad_scores, key_heads, preferred_element_type=jnp.float32)
            * score_scale
        )
        grad_keys = grad_keys + jnp.einsum(
            "hbk,bhd->khd", grad_scores, query_block, preferred_element_type=jnp.float32
        )
        return (
            (grad_keys, grad_values),
            grad_query.astype(jnp.bfloat16).reshape(block_rows, head_cols),
        )

    empty_sum = jnp.zeros((length, head_count, HD), jnp.float32)
    (grad_keys, grad_values), grad_query = lax.scan(
        one_block,
        (empty_sum, empty_sum),
        (
            query_heads.reshape(block_count, block_rows, head_count, HD),
            segment.reshape(block_count, block_rows),
            grad_context.reshape(block_count, block_rows, head_count, HD),
            log_total,
        ),
    )
    grad_keys = (grad_keys * score_scale).astype(jnp.bfloat16).reshape(length, head_cols)
    grad_values = grad_values.astype(jnp.bfloat16).reshape(length, head_cols)
    return (grad_query.reshape(length, head_cols), grad_keys, grad_values)


def exchange(blocks, axis):
    count = blocks.shape[0]
    me = lax.axis_index(axis)
    got = [lax.dynamic_index_in_dim(blocks, me, axis=0, keepdims=False)]
    for step in range(1, count):
        piece = lax.dynamic_index_in_dim(blocks, (me + step) % count, axis=0, keepdims=False)
        pairs = [(source, (source + step) % count) for source in range(count)]
        got.append(lax.ppermute(piece, axis, pairs))
    order = (me - jnp.arange(count)) % count
    return jnp.take(jnp.stack(got), order, axis=0)


def split_columns(values, axis):
    count = lax.axis_size(axis)
    rows, cols = values.shape
    blocks = values.reshape(rows, count, cols // count).transpose(1, 0, 2)
    return exchange(blocks, axis).reshape(count * rows, cols // count)


def seq_gathered_grad(left, right):
    left_all = lax.all_gather(left, "seq", axis=0, tiled=True)
    right_cols = split_columns(right, "seq")
    partial = contract_rows(left_all, right_cols)
    return lax.psum_scatter(partial, "batch", scatter_dimension=0, tiled=True)


def batch_gathered_grad(left, right):
    left_rows = split_columns(left, "batch")
    right_all = lax.all_gather(right, "batch", axis=0, tiled=True)
    partial = contract_rows(left_rows, right_all)
    return lax.psum_scatter(partial, "seq", scatter_dimension=1, tiled=True)


GRAD_PLAN = {"skip": "batch", "qkv": "seq", "out": "batch", "hidden": "seq", "down": "batch"}


def weight_grad(name, left, right):
    if GRAD_PLAN[name] == "seq":
        return seq_gathered_grad(left, right)
    return batch_gathered_grad(left, right)


def on_device(
    tokens,
    long_skip,
    lengths,
    skip_weight,
    skip_bias,
    attention_gain,
    attention_shift,
    qkv_weight,
    out_weight,
    out_bias,
    mlp_gain,
    mlp_shift,
    hidden_weight,
    hidden_bias,
    down_weight,
    down_bias,
    cotangent,
):
    local_rows = tokens.shape[1]
    feature_count = tokens.shape[2]
    group_len = local_rows * lax.axis_size("seq")
    joined = jnp.concatenate([tokens[0], long_skip[0]], axis=1)
    mixed = product(joined, skip_weight) + skip_bias.astype(jnp.float32)
    normed_full, first_pull = jax.vjp(
        layer_norm, mixed, attention_gain.astype(jnp.float32), attention_shift.astype(jnp.float32)
    )
    normed_one = normed_full.astype(jnp.bfloat16)
    packed = product(normed_one, qkv_weight).astype(jnp.bfloat16)
    seq_count = lax.axis_size("seq")
    packed_heads = lax.all_to_all(
        packed.reshape(local_rows, 3, seq_count, feature_count // seq_count),
        "seq",
        split_axis=2,
        concat_axis=0,
        tiled=True,
    ).reshape(group_len, 3, feature_count // seq_count)
    query_heads = packed_heads[:, 0]
    key_heads = packed_heads[:, 1]
    value_heads = packed_heads[:, 2]
    segment = segments(lengths[0], group_len)
    context_heads, log_total = attend_forward(query_heads, key_heads, value_heads, segment)
    context_tok = lax.all_to_all(context_heads, "seq", split_axis=0, concat_axis=1, tiled=True)
    middle = mixed + product(context_tok, out_weight) + out_bias.astype(jnp.float32)
    second_full, second_pull = jax.vjp(
        layer_norm, middle, mlp_gain.astype(jnp.float32), mlp_shift.astype(jnp.float32)
    )
    normed_two = second_full.astype(jnp.bfloat16)
    hidden_pre = product(normed_two, hidden_weight) + hidden_bias.astype(jnp.float32)
    act_full, gelu_pull = jax.vjp(exact_gelu, hidden_pre)
    hidden_act = act_full.astype(jnp.bfloat16)
    output = (middle + product(hidden_act, down_weight) + down_bias.astype(jnp.float32)).astype(
        jnp.bfloat16
    )
    grad_out_rows = cotangent[0]
    grad_down_weight = weight_grad("down", hidden_act, grad_out_rows)
    grad_down_bias = column_sums(grad_out_rows)
    grad_act = times_transposed(grad_out_rows, down_weight)
    grad_pre = gelu_pull(grad_act)[0].astype(jnp.bfloat16)
    grad_hidden_weight = weight_grad("hidden", normed_two, grad_pre)
    grad_hidden_bias = column_sums(grad_pre)
    grad_normed_two = times_transposed(grad_pre, hidden_weight)
    grad_middle_norm, grad_mlp_gain, grad_mlp_shift = second_pull(grad_normed_two)
    grad_middle = grad_out_rows.astype(jnp.float32) + grad_middle_norm
    grad_attended = grad_middle.astype(jnp.bfloat16)
    grad_out_bias = column_sums(grad_attended)
    grad_out_weight = weight_grad("out", context_tok, grad_attended)
    grad_context = times_transposed(grad_attended, out_weight).astype(jnp.bfloat16)
    grad_context_heads = lax.all_to_all(
        grad_context, "seq", split_axis=1, concat_axis=0, tiled=True
    )
    grad_query, grad_key, grad_value = attend_backward(
        query_heads, key_heads, value_heads, segment, grad_context_heads, log_total
    )
    grad_packed = lax.all_to_all(
        jnp.stack([grad_query, grad_key, grad_value], axis=1)[:, :, None],
        "seq",
        split_axis=0,
        concat_axis=2,
        tiled=True,
    ).reshape(local_rows, 3 * feature_count)
    grad_qkv_weight = weight_grad("qkv", normed_one, grad_packed)
    grad_normed_one = times_transposed(grad_packed, qkv_weight)
    grad_mixed_norm, grad_attention_gain, grad_attention_shift = first_pull(grad_normed_one)
    grad_mixed = (grad_middle + grad_mixed_norm).astype(jnp.bfloat16)
    grad_skip_bias = column_sums(grad_mixed)
    grad_skip_weight = weight_grad("skip", joined, grad_mixed)
    grad_joined = times_transposed(grad_mixed, skip_weight)
    grad_tokens = grad_joined[:, :feature_count][None]
    grad_long_skip = grad_joined[:, feature_count:][None]
    summed_weights = (
        grad_skip_weight,
        grad_qkv_weight,
        grad_out_weight,
        grad_hidden_weight,
        grad_down_weight,
    )
    small_grads = (
        grad_skip_bias,
        grad_attention_gain,
        grad_attention_shift,
        grad_out_bias,
        grad_mlp_gain,
        grad_mlp_shift,
        grad_hidden_bias,
        grad_down_bias,
    )
    small_sizes = [piece.shape[0] for piece in small_grads]
    small_total = lax.psum(jnp.concatenate(small_grads), ("seq", "batch"))
    summed_small = []
    offset = 0
    for size in small_sizes:
        summed_small.append(small_total[offset : offset + size])
        offset += size
    return (
        output[None],
        grad_tokens,
        grad_long_skip,
        summed_weights[0],
        summed_small[0],
        summed_small[1],
        summed_small[2],
        summed_weights[1],
        summed_weights[2],
        summed_small[3],
        summed_small[4],
        summed_small[5],
        summed_weights[3],
        summed_small[6],
        summed_weights[4],
        summed_small[7],
    )


def solution(mesh):
    in_specs = (
        P("batch", "seq", None),
        P("batch", "seq", None),
        P("batch", None),
        P(),
        P(),
        P(),
        P(),
        P(),
        P(),
        P(),
        P(),
        P(),
        P(),
        P(),
        P(),
        P(),
        P("batch", "seq", None),
    )
    out_specs = (
        P("batch", "seq", None),
        P("batch", "seq", None),
        P("batch", "seq", None),
        P("batch", "seq"),
        P(),
        P(),
        P(),
        P("batch", "seq"),
        P("batch", "seq"),
        P(),
        P(),
        P(),
        P("batch", "seq"),
        P(),
        P("batch", "seq"),
        P(),
    )
    return jax.shard_map(
        on_device, mesh=mesh, in_specs=in_specs, out_specs=out_specs, check_vma=False
    )
```

profile of v0, /device:TPU:0, one launch (start us, length us, event | category | flops | bytes accessed | tf_op | source)
XLA Modules:
  0.0 813.6 jit_solution(7529825776939285861)
XLA Ops:
  14.6 7.2 convolution_convert_fusion
  28.5 6.8 all-to-all-start
  35.6 41.7 %all-to-all-done = bf16[256,3,8,144]{0,3,1,2:T(8,128)(2,1)} async-done(((bf16[256,3,8,144]{0,3,1,2:T(8,128)(2,1)}), bf16[256,3,8,144]{0,3,1,2:T(8,128)(2,1)}, u32[]{:S(2)}, u32[]{:S(2)}) %all-to-all-start) | async-done | bytes 1769504 | tf_op jit(solution)/shard_map/all_to_all | solution.py:207
  92.6 36.5 %while.27 = (s32[]{:T(128)}, bf16[4,512,144]{1,2,0:T(8,128)(2,1)}, f32[4,2,512,1]{2,1,3,0:T(2,128)S(1)}, s32[4,512]{1,0:T(4,128)S(1)}, s32[2048]{0:T(1024)S(1)},...) while((s32[]{:T(128)}, bf16[4,512,144]{1,2,0:T(8,128)(2,1)}, ...), condition=%wide.region_7.8_spmd, body=%wide.region_4.7_spmd.sunk | while | flops 628169728 | bytes 33537152 | solution.py:74
  140.6 16.1 %all-to-all-done.1 = bf16[8,256,144]{1,2,0:T(8,128)(2,1)} async-done(((bf16[8,256,144]{1,2,0:T(8,128)(2,1)}), bf16[8,256,144]{1,2,0:T(8,128)(2,1)}, u32[]{:S(2)}, u32[]{:S(2)}) %all-to-all-start.1) | async-done | bytes 589856 | tf_op jit(solution)/shard_map/all_to_all | solution.py:219
  161.4 17.1 %multiply_convert_fusion.1 = (bf16[256,4608]{1,0:T(8,128)(2,1)}, f32[256,4608]{1,0:T(8,128)}, f32[256,4608]{1,0:T(8,128)}) fusion(f32[4608]{0:T(1024)S(1)} %convert_element_type.104, bf16[256,1152]{1,0:T(8,128)(2,1)} %add_convert_fusion.2, bf16[1152,4608]{1,0:T(8,128)(2,1)} %param.33), kind=kOutput, calls=%fused_computation.61 | convolution fusion | flops 2795765760 | bytes 23021568 | tf_op jit(solution)/shard_map/dot_general | solution.py:12
  178.5 14.6 %convert_reduce_fusion = (f32[4608]{0:T(1024)}, bf16[256,4608]{1,0:T(8,128)(2,1)}) fusion(f32[256,4608]{1,0:T(8,128)} %get-tuple-element.309, f32[256,4608]{1,0:T(8,128)} %get-tuple-element.357, bf16[4608,1152]{1,0:T(8,128)(2,1)} %param.35, bf16[1,256,1152]{2,1,0:T(8,128)(2,1)S(1)} %copy-done.13), kind=kOutput, calls=%fused_computation.59 | convolution fusion | flops 2736778752 | bytes 23021568 | tf_op jit(solution)/shard_map/dot_general | solution.py:22
  193.2 8.7 %multiply_reduce_fusion.1 = (f32[1152]{0:T(1024)}, f32[256]{0:T(256)S(1)}, f32[1152]{0:T(1024)}, f32[256,1152]{1,0:T(8,128)S(1)}) fusion(f32[256,1152]{1,0:T(8,128)S(1)} %copy-done.7, f32[256]{0:T(256)S(1)} %fusion.83, f32[256]{0:T(256)S(1)} %broadcast_multiply_fusion, f32[1152]{0:T(1024)S(1)} %convert_element_type.101, ...), kind=kOutput, calls=%fused_computation.113 | convolution fusion | flops 2720265728 | bytes 15352320 | tf_op jit(solution)/shard_map/dot_general | solution.py:22
  214.5 15.9 %all-to-all-done.2 = bf16[256,8,144]{0,2,1:T(8,128)(2,1)S(1)} async-done(((bf16[256,8,144]{0,2,1:T(8,128)(2,1)}), bf16[256,8,144]{0,2,1:T(8,128)(2,1)S(1)}, u32[]{:S(2)}, u32[]{:S(2)}) %all-to-all-start.2) | async-done | bytes 589856 | tf_op jit(solution)/shard_map/all_to_all | solution.py:245
  232.7 96.8 %while.28 = (s32[]{:T(128)}, f32[2048,2,72]{0,2,1:T(8,128)S(1)}, f32[2048,2,72]{0,2,1:T(8,128)}, bf16[4,512,144]{1,2,0:T(8,128)(2,1)}, bf16[4,512,2,72]{1,3,2,0:...) while((s32[]{:T(128)}, f32[2048,2,72]{0,2,1:T(8,128)S(1)}, ...), condition=%wide.region_14.15_spmd.clone, body=%wide.region_12.14_spmd.clone.sunk | while | flops 1543781376 | bytes 144143088 | solution.py:120
  337.9 8.6 %reshape.483 = bf16[8,2,55296]{2,1,0:T(2,128)(2,1)} reshape(bf16[2048,1,3,144]{3,2,1,0:T(4,128)(2,1)} %bitcast.291) | data formatting | bytes 3538944
  351.0 41.1 %all-to-all-done.3 = bf16[8,2,55296]{2,1,0:T(2,128)(2,1)S(1)} async-done(((bf16[8,2,55296]{2,1,0:T(2,128)(2,1)}), bf16[8,2,55296]{2,1,0:T(2,128)(2,1)S(1)}, u32[]{:S(2)}, u32[]{:S(2)}) %all-to-all-start.3) | async-done | bytes 1769504 | tf_op jit(solution)/shard_map/all_to_all | solution.py:251
  392.2 6.8 reshape.484
  399.0 6.9 copy.151
  406.0 6.6 multiply_reduce_fusion.2
  457.0 22.1 %collective-permute-done.5 = bf16[256,432]{0,1:T(8,128)(2,1)S(1)} collective-permute-done((bf16[256,432]{0,1:T(8,128)(2,1)S(1)}, bf16[256,432]{0,1:T(8,128)(2,1)S(1)}, u32[]{:S(2)}, u32[]{:S(2)}) %collective-permute-start.5) | collective-permute-done | bytes 221216 | tf_op jit(solution)/shard_map/ppermute | solution.py:142
  486.3 7.0 fusion.53
  505.2 7.2 collective-permute-done.20
  512.4 6.2 collective-permute-done.21
  525.0 8.0 fusion.48
  546.8 5.4 fusion.60
  555.5 13.3 %collective-permute-start.13 = (bf16[256,576]{0,1:T(8,128)(2,1)S(1)}, bf16[256,576]{0,1:T(8,128)(2,1)S(1)}, u32[]{:S(2)}, u32[]{:S(2)}) collective-permute-start(bf16[256,576]{0,1:T(8,128)(2,1)S(1)} %get-tuple-element.324), channel_id=1, source_target_pairs={{0,4},{4,8},{8,12},{12,16},{16,20},{20,24},{24,28},{28,0},{1,5},{5... | collective-permute-start | bytes 884744 | tf_op jit(solution)/shard_map/ppermute | solution.py:142
  568.8 37.8 %collective-permute-start.14 = (bf16[256,576]{0,1:T(8,128)(2,1)S(1)}, bf16[256,576]{0,1:T(8,128)(2,1)S(1)}, u32[]{:S(2)}, u32[]{:S(2)}) collective-permute-start(bf16[256,576]{0,1:T(8,128)(2,1)S(1)} %get-tuple-element.323), channel_id=1, source_target_pairs={{0,8},{4,12},{8,16},{12,20},{16,24},{20,28},{24,0},{28,4},{1,9},{5... | collective-permute-start | bytes 884744 | tf_op jit(solution)/shard_map/ppermute | solution.py:142
  607.4 9.8 %collective-permute-start.15 = (bf16[256,576]{0,1:T(8,128)(2,1)S(1)}, bf16[256,576]{0,1:T(8,128)(2,1)S(1)}, u32[]{:S(2)}, u32[]{:S(2)}) collective-permute-start(bf16[256,576]{0,1:T(8,128)(2,1)S(1)} %get-tuple-element.322), channel_id=1, source_target_pairs={{0,12},{4,16},{8,20},{12,24},{16,28},{20,0},{24,4},{28,8},{1,13},{... | collective-permute-start | bytes 884744 | tf_op jit(solution)/shard_map/ppermute | solution.py:142
  623.0 9.8 %collective-permute-start.19 = (bf16[256,576]{0,1:T(8,128)(2,1)S(1)}, bf16[256,576]{0,1:T(8,128)(2,1)S(1)}, u32[]{:S(2)}, u32[]{:S(2)}) collective-permute-start(bf16[256,576]{0,1:T(8,128)(2,1)S(1)} %get-tuple-element.318), channel_id=1, source_target_pairs={{0,28},{4,0},{8,4},{12,8},{16,12},{20,16},{24,20},{28,24},{1,29},{... | collective-permute-start | bytes 884744 | tf_op jit(solution)/shard_map/ppermute | solution.py:142
  634.2 17.3 %collective-permute-done.16 = bf16[256,576]{0,1:T(8,128)(2,1)S(1)} collective-permute-done((bf16[256,576]{0,1:T(8,128)(2,1)S(1)}, bf16[256,576]{0,1:T(8,128)(2,1)S(1)}, u32[]{:S(2)}, u32[]{:S(2)}) %collective-permute-start.16) | collective-permute-done | bytes 294944 | tf_op jit(solution)/shard_map/ppermute | solution.py:142
  655.5 11.4 %collective-permute-done.18 = bf16[256,576]{0,1:T(8,128)(2,1)S(1)} collective-permute-done((bf16[256,576]{0,1:T(8,128)(2,1)S(1)}, bf16[256,576]{0,1:T(8,128)(2,1)S(1)}, u32[]{:S(2)}, u32[]{:S(2)}) %collective-permute-start.18) | collective-permute-done | bytes 294944 | tf_op jit(solution)/shard_map/ppermute | solution.py:142
  667.7 10.9 %collective-permute-done.19 = bf16[256,576]{0,1:T(8,128)(2,1)S(1)} collective-permute-done((bf16[256,576]{0,1:T(8,128)(2,1)S(1)}, bf16[256,576]{0,1:T(8,128)(2,1)S(1)}, u32[]{:S(2)}, u32[]{:S(2)}) %collective-permute-start.19) | collective-permute-done | bytes 294944 | tf_op jit(solution)/shard_map/ppermute | solution.py:142
  683.5 8.6 %fusion.50 = f32[1152,576]{1,0:T(8,128)} fusion(bf16[2048,1152]{1,0:T(8,128)(2,1)} %all-gather.13.cloned.1.call-done, bf16[2048,576]{0,1:T(8,128)(2,1)} %bitcast.307, pred[2048]{0:T(1024)(128)(4,1)S(1)} %broadcast_in_dim.155), kind=kOutput, calls=%fused_computation.87 | convolution fusion | flops 2719088640 | bytes 9734144 | tf_op jit(solution)/shard_map/dot_general | solution.py:16
  693.4 8.9 %fusion.47 = bf16[1,256,1152]{2,1,0:T(8,128)(2,1)} fusion(f32[256,1152]{1,0:T(8,128)S(1)} %copy-done.8, bf16[256,4608]{1,0:T(8,128)(2,1)} %get-tuple-element.308, bf16[4608,1152]{1,0:T(8,128)(2,1)} %param.35, f32[1152]{0:T(1024)S(1)} %convert_element_type.106), kind=kOutput, calls=%fused_computation.82 | convolution fusion | flops 2718793728 | bytes 14750208 | tf_op jit(solution)/shard_map/dot_general | solution.py:12
  702.5 64.8 %psum.7 = f32[12672]{0:T(1024)S(1)} all-reduce(f32[12672]{0:T(1024)S(1)} %constant_dynamic-update-slice_fusion.1), channel_id=1, replica_groups=mesh['seq'=8,'batch'=4] {'seq','batch'}, use_global_device_ids=true, to_apply=%region_26.27 | all-reduce | flops 12672 | bytes 101376 | tf_op jit(solution)/shard_map/psum | solution.py:285
  774.8 31.7 %reduce-scatter.12.cloned.1.call-done = f32[288,576]{1,0:T(8,128)} async-done(((f32[1152,576]{1,0:T(8,128)}), f32[288,576]{1,0:T(8,128)}) %reduce-scatter.12.cloned.1.call-update) | async-done | bytes 663568 | tf_op jit(solution)/shard_map/reduce_scatter | solution.py:158
  (361 shorter events, 319.3 us)
Async XLA Ops:
  28.5 48.9 %all-to-all-start = ((bf16[256,3,8,144]{0,3,1,2:T(8,128)(2,1)}), bf16[256,3,8,144]{0,3,1,2:T(8,128)(2,1)}, u32[]{:S(2)}, u32[]{:S(2)}) async-start(bf16[256,3,8,144]{0,3,1,2:T(8,128)(2,1)} %copy.125), calls=%async_computation | async-start | bytes 3538944 | tf_op jit(solution)/shard_map/all_to_all | solution.py:207
  135.8 20.9 %all-to-all-start.1 = ((bf16[8,256,144]{1,2,0:T(8,128)(2,1)}), bf16[8,256,144]{1,2,0:T(8,128)(2,1)}, u32[]{:S(2)}, u32[]{:S(2)}) async-start(bf16[8,256,144]{1,2,0:T(8,128)(2,1)} %copy.129), calls=%async_computation.1 | async-start | bytes 1179648 | tf_op jit(solution)/shard_map/all_to_all | solution.py:219
  140.0 290.8 %all-gather.11.cloned.1.call-start = ((), (), s32[]{:S(2)}) async-start(), calls=%async_computation.13 | async-start | bytes 2949120 | tf_op jit(solution)/shard_map/all_gather | solution.py:163
  210.1 20.2 %all-to-all-start.2 = ((bf16[256,8,144]{0,2,1:T(8,128)(2,1)}), bf16[256,8,144]{0,2,1:T(8,128)(2,1)S(1)}, u32[]{:S(2)}, u32[]{:S(2)}) async-start(bf16[256,8,144]{0,2,1:T(8,128)(2,1)} %bitcast.18), calls=%async_computation.2 | async-start | bytes 1179648 | tf_op jit(solution)/shard_map/all_to_all | solution.py:245
  213.7 272.6 %all-gather.9.cloned.1.call-start = ((), (), s32[]{:S(2)}) async-start(), calls=%async_computation.11 | async-start | bytes 5308416 | tf_op jit(solution)/shard_map/all_gather | solution.py:155
  346.4 45.7 %all-to-all-start.3 = ((bf16[8,2,55296]{2,1,0:T(2,128)(2,1)}), bf16[8,2,55296]{2,1,0:T(2,128)(2,1)S(1)}, u32[]{:S(2)}, u32[]{:S(2)}) async-start(bf16[8,2,55296]{2,1,0:T(2,128)(2,1)} %reshape.483), calls=%async_computation.3 | async-start | bytes 3538944 | tf_op jit(solution)/shard_map/all_to_all | solution.py:251
  350.3 174.7 %all-gather.15.cloned.1.call-start = ((), (), s32[]{:S(2)}) async-start(), calls=%async_computation.18 | async-start | bytes 2949120 | tf_op jit(solution)/shard_map/all_gather | solution.py:163
  351.0 195.8 %all-gather.7.cloned.1.call-start = ((), (), s32[]{:S(2)}) async-start(), calls=%async_computation.9 | async-start | bytes 2949120 | tf_op jit(solution)/shard_map/all_gather | solution.py:163
  415.2 268.3 %all-gather.13.cloned.1.call-start = ((), (), s32[]{:S(2)}) async-start(), calls=%async_computation.15 | async-start | bytes 5308416 | tf_op jit(solution)/shard_map/all_gather | solution.py:155
  415.8 359.0 %reduce-scatter.10.cloned.1.call-start = ((), (), s32[]{:S(2)}) async-start(), calls=%async_computation.14 | async-start | bytes 1990656 | tf_op jit(solution)/shard_map/reduce_scatter | solution.py:165
  418.6 9.8 %collective-permute-start.11 = (bf16[256,288]{0,1:T(8,128)(2,1)S(1)}, bf16[256,288]{0,1:T(8,128)(2,1)S(1)}, u32[]{:S(2)}, u32[]{:S(2)}) collective-permute-start(bf16[256,288]{0,1:T(8,128)(2,1)S(1)} %get-tuple-element.343), channel_id=1, source_target_pairs={{0,2},{1,3},{2,0},{3,1},{4,6},{5,7},{6,4},{7,5},{8,10},{9,11},{10,... | collective-permute-start | bytes 442376 | tf_op jit(solution)/shard_map/ppermute | solution.py:142
  420.1 9.9 %collective-permute-start.12 = (bf16[256,288]{0,1:T(8,128)(2,1)S(1)}, bf16[256,288]{0,1:T(8,128)(2,1)S(1)}, u32[]{:S(2)}, u32[]{:S(2)}) collective-permute-start(bf16[256,288]{0,1:T(8,128)(2,1)S(1)} %get-tuple-element.342), channel_id=1, source_target_pairs={{0,3},{1,0},{2,1},{3,2},{4,7},{5,4},{6,5},{7,6},{8,11},{9,8},{10,9... | collective-permute-start | bytes 442376 | tf_op jit(solution)/shard_map/ppermute | solution.py:142
  435.3 339.6 %reduce-scatter.8.cloned.1.call-start = ((), (), s32[]{:S(2)}) async-start(), calls=%async_computation.12 | async-start | bytes 2949120 | tf_op jit(solution)/shard_map/reduce_scatter | solution.py:158
  442.7 10.3 %collective-permute-start.4 = (bf16[256,432]{0,1:T(8,128)(2,1)S(1)}, bf16[256,432]{0,1:T(8,128)(2,1)S(1)}, u32[]{:S(2)}, u32[]{:S(2)}) collective-permute-start(bf16[256,432]{0,1:T(8,128)(2,1)S(1)} %get-tuple-element.332), channel_id=1, source_target_pairs={{0,8},{4,12},{8,16},{12,20},{16,24},{20,28},{24,0},{28,4},{1,9},{5... | collective-permute-start | bytes 663560 | tf_op jit(solution)/shard_map/ppermute | solution.py:142
  442.7 36.4 %collective-permute-start.5 = (bf16[256,432]{0,1:T(8,128)(2,1)S(1)}, bf16[256,432]{0,1:T(8,128)(2,1)S(1)}, u32[]{:S(2)}, u32[]{:S(2)}) collective-permute-start(bf16[256,432]{0,1:T(8,128)(2,1)S(1)} %get-tuple-element.331), channel_id=1, source_target_pairs={{0,12},{4,16},{8,20},{12,24},{16,28},{20,0},{24,4},{28,8},{1,13},{... | collective-permute-start | bytes 663560 | tf_op jit(solution)/shard_map/ppermute | solution.py:142
  443.1 36.8 %collective-permute-start.6 = (bf16[256,432]{0,1:T(8,128)(2,1)S(1)}, bf16[256,432]{0,1:T(8,128)(2,1)S(1)}, u32[]{:S(2)}, u32[]{:S(2)}) collective-permute-start(bf16[256,432]{0,1:T(8,128)(2,1)S(1)} %get-tuple-element.330), channel_id=1, source_target_pairs={{0,16},{4,20},{8,24},{12,28},{16,0},{20,4},{24,8},{28,12},{1,17},{... | collective-permute-start | bytes 663560 | tf_op jit(solution)/shard_map/ppermute | solution.py:142
  446.8 33.7 %collective-permute-start.7 = (bf16[256,432]{0,1:T(8,128)(2,1)S(1)}, bf16[256,432]{0,1:T(8,128)(2,1)S(1)}, u32[]{:S(2)}, u32[]{:S(2)}) collective-permute-start(bf16[256,432]{0,1:T(8,128)(2,1)S(1)} %get-tuple-element.329), channel_id=1, source_target_pairs={{0,20},{4,24},{8,28},{12,0},{16,4},{20,8},{24,12},{28,16},{1,21},{... | collective-permute-start | bytes 663560 | tf_op jit(solution)/shard_map/ppermute | solution.py:142
  451.7 29.5 %collective-permute-start.8 = (bf16[256,432]{0,1:T(8,128)(2,1)S(1)}, bf16[256,432]{0,1:T(8,128)(2,1)S(1)}, u32[]{:S(2)}, u32[]{:S(2)}) collective-permute-start(bf16[256,432]{0,1:T(8,128)(2,1)S(1)} %get-tuple-element.328), channel_id=1, source_target_pairs={{0,24},{4,28},{8,0},{12,4},{16,8},{20,12},{24,16},{28,20},{1,25},{... | collective-permute-start | bytes 663560 | tf_op jit(solution)/shard_map/ppermute | solution.py:142
  453.0 28.9 %collective-permute-start.9 = (bf16[256,432]{0,1:T(8,128)(2,1)S(1)}, bf16[256,432]{0,1:T(8,128)(2,1)S(1)}, u32[]{:S(2)}, u32[]{:S(2)}) collective-permute-start(bf16[256,432]{0,1:T(8,128)(2,1)S(1)} %get-tuple-element.327), channel_id=1, source_target_pairs={{0,28},{4,0},{8,4},{12,8},{16,12},{20,16},{24,20},{28,24},{1,29},{... | collective-permute-start | bytes 663560 | tf_op jit(solution)/shard_map/ppermute | solution.py:142
  493.3 281.5 %reduce-scatter.14.cloned.1.call-start = ((), (), s32[]{:S(2)}) async-start(), calls=%async_computation.17 | async-start | bytes 5971968 | tf_op jit(solution)/shard_map/reduce_scatter | solution.py:165
  501.4 10.9 %collective-permute-start.20 = (bf16[256,1152]{1,0:T(8,128)(2,1)S(1)}, bf16[256,1152]{1,0:T(8,128)(2,1)S(1)}, u32[]{:S(2)}, u32[]{:S(2)}) collective-permute-start(bf16[256,1152]{1,0:T(8,128)(2,1)S(1)} %bitcast.317), channel_id=1, source_target_pairs={{0,1},{1,2},{2,3},{3,0},{4,5},{5,6},{6,7},{7,4},{8,9},{9,10},{10,1... | collective-permute-start | bytes 1769480 | tf_op jit(solution)/shard_map/ppermute | solution.py:142
  503.1 15.5 %collective-permute-start.21 = (bf16[256,1152]{1,0:T(8,128)(2,1)S(1)}, bf16[256,1152]{1,0:T(8,128)(2,1)S(1)}, u32[]{:S(2)}, u32[]{:S(2)}) collective-permute-start(bf16[256,1152]{1,0:T(8,128)(2,1)S(1)} %bitcast.318), channel_id=1, source_target_pairs={{0,2},{1,3},{2,0},{3,1},{4,6},{5,7},{6,4},{7,5},{8,10},{9,11},{10,... | collective-permute-start | bytes 1769480 | tf_op jit(solution)/shard_map/ppermute | solution.py:142
  503.3 15.3 %collective-permute-start.22 = (bf16[256,1152]{1,0:T(8,128)(2,1)S(1)}, bf16[256,1152]{1,0:T(8,128)(2,1)S(1)}, u32[]{:S(2)}, u32[]{:S(2)}) collective-permute-start(bf16[256,1152]{1,0:T(8,128)(2,1)S(1)} %bitcast.319), channel_id=1, source_target_pairs={{0,3},{1,0},{2,1},{3,2},{4,7},{5,4},{6,5},{7,6},{8,11},{9,8},{10,9... | collective-permute-start | bytes 1769480 | tf_op jit(solution)/shard_map/ppermute | solution.py:142
  533.0 241.8 %reduce-scatter.6.cloned.1.call-start = ((), (), s32[]{:S(2)}) async-start(), calls=%async_computation.10 | async-start | bytes 3317760 | tf_op jit(solution)/shard_map/reduce_scatter | solution.py:165
  552.3 254.2 %reduce-scatter.12.cloned.1.call-start = ((), (), s32[]{:S(2)}) async-start(), calls=%async_computation.16 | async-start | bytes 3686400 | tf_op jit(solution)/shard_map/reduce_scatter | solution.py:158
  555.5 64.0 %collective-permute-start.13 = (bf16[256,576]{0,1:T(8,128)(2,1)S(1)}, bf16[256,576]{0,1:T(8,128)(2,1)S(1)}, u32[]{:S(2)}, u32[]{:S(2)}) collective-permute-start(bf16[256,576]{0,1:T(8,128)(2,1)S(1)} %get-tuple-element.324), channel_id=1, source_target_pairs={{0,4},{4,8},{8,12},{12,16},{16,20},{20,24},{24,28},{28,0},{1,5},{5... | collective-permute-start | bytes 884744 | tf_op jit(solution)/shard_map/ppermute | solution.py:142
  568.8 54.2 %collective-permute-start.14 = (bf16[256,576]{0,1:T(8,128)(2,1)S(1)}, bf16[256,576]{0,1:T(8,128)(2,1)S(1)}, u32[]{:S(2)}, u32[]{:S(2)}) collective-permute-start(bf16[256,576]{0,1:T(8,128)(2,1)S(1)} %get-tuple-element.323), channel_id=1, source_target_pairs={{0,8},{4,12},{8,16},{12,20},{16,24},{20,28},{24,0},{28,4},{1,9},{5... | collective-permute-start | bytes 884744 | tf_op jit(solution)/shard_map/ppermute | solution.py:142
  607.4 26.1 %collective-permute-start.15 = (bf16[256,576]{0,1:T(8,128)(2,1)S(1)}, bf16[256,576]{0,1:T(8,128)(2,1)S(1)}, u32[]{:S(2)}, u32[]{:S(2)}) collective-permute-start(bf16[256,576]{0,1:T(8,128)(2,1)S(1)} %get-tuple-element.322), channel_id=1, source_target_pairs={{0,12},{4,16},{8,20},{12,24},{16,28},{20,0},{24,4},{28,8},{1,13},{... | collective-permute-start | bytes 884744 | tf_op jit(solution)/shard_map/ppermute | solution.py:142
  617.2 34.4 %collective-permute-start.16 = (bf16[256,576]{0,1:T(8,128)(2,1)S(1)}, bf16[256,576]{0,1:T(8,128)(2,1)S(1)}, u32[]{:S(2)}, u32[]{:S(2)}) collective-permute-start(bf16[256,576]{0,1:T(8,128)(2,1)S(1)} %get-tuple-element.321), channel_id=1, source_target_pairs={{0,16},{4,20},{8,24},{12,28},{16,0},{20,4},{24,8},{28,12},{1,17},{... | collective-permute-start | bytes 884744 | tf_op jit(solution)/shard_map/ppermute | solution.py:142
  617.2 37.6 %collective-permute-start.17 = (bf16[256,576]{0,1:T(8,128)(2,1)S(1)}, bf16[256,576]{0,1:T(8,128)(2,1)S(1)}, u32[]{:S(2)}, u32[]{:S(2)}) collective-permute-start(bf16[256,576]{0,1:T(8,128)(2,1)S(1)} %get-tuple-element.320), channel_id=1, source_target_pairs={{0,20},{4,24},{8,28},{12,0},{16,4},{20,8},{24,12},{28,16},{1,21},{... | collective-permute-start | bytes 884744 | tf_op jit(solution)/shard_map/ppermute | solution.py:142
  619.5 47.4 %collective-permute-start.18 = (bf16[256,576]{0,1:T(8,128)(2,1)S(1)}, bf16[256,576]{0,1:T(8,128)(2,1)S(1)}, u32[]{:S(2)}, u32[]{:S(2)}) collective-permute-start(bf16[256,576]{0,1:T(8,128)(2,1)S(1)} %get-tuple-element.319), channel_id=1, source_target_pairs={{0,24},{4,28},{8,0},{12,4},{16,8},{20,12},{24,16},{28,20},{1,25},{... | collective-permute-start | bytes 884744 | tf_op jit(solution)/shard_map/ppermute | solution.py:142
  623.0 55.6 %collective-permute-start.19 = (bf16[256,576]{0,1:T(8,128)(2,1)S(1)}, bf16[256,576]{0,1:T(8,128)(2,1)S(1)}, u32[]{:S(2)}, u32[]{:S(2)}) collective-permute-start(bf16[256,576]{0,1:T(8,128)(2,1)S(1)} %get-tuple-element.318), channel_id=1, source_target_pairs={{0,28},{4,0},{8,4},{12,8},{16,12},{20,16},{24,20},{28,24},{1,29},{... | collective-permute-start | bytes 884744 | tf_op jit(solution)/shard_map/ppermute | solution.py:142
  (56 other events, 564.9 us)
Sparse Core Ops, SparseCore 0:
  205.2 36.2 all-gather.10
  243.1 51.1 all-gather.8
  352.9 38.6 all-gather.14
  415.3 36.7 all-gather.6
  453.6 71.3 all-gather.12
  527.7 32.4 reduce-scatter.9
  563.9 43.4 reduce-scatter.7
  610.2 103.6 reduce-scatter.13
  716.8 44.0 reduce-scatter.5
  764.4 42.0 reduce-scatter.11
where the time goes:
time: 820 us; the launch traced here: 814 us
  waiting for transfers between devices  246 us (30%)
  matrix products  208 us (25%)
  local copies, waits for them, and re-layouts  120 us (15%)
  starting transfers between devices  115 us (14%)
  blocking collectives  64.8 us (8%)
  other arithmetic  43.7 us (5%)
  between operations  15.3 us (2%)
    ppermute x23, waiting for transfers between devices, exchange(): got.append(lax.ppermute(piece, axis, pairs))  97.9 us
    ppermute x23, starting transfers between devices, exchange(): got.append(lax.ppermute(piece, axis, pairs))  94.7 us
    psum x1, blocking collectives, on_device(): small_total = lax.psum(jnp.concatenate(small_grads), ('seq', 'batch'))  64.8 us
    all_to_all x1, waiting for transfers between devices, on_device(): lax.all_to_all(packed.reshape(local_rows, 3, seq_count, feature_count //...  41.7 us
    all_to_all x1, waiting for transfers between devices, on_device(): lax.all_to_all(jnp.stack([grad_query, grad_key, grad_value], axis=1)[:, :...  41.1 us
    dot_general x5, matrix products, product(): return jnp.dot(left, right, preferred_element_type=jnp.float32)  40.5 us
    dot_general x5, matrix products, times_transposed(): lax.dot_general(left, right, (((1,), (1,)), ((), ())), preferred_element_...  37.6 us
    unnamed x100, local copies, waits for them, and re-layouts  33.6 us
  transfers between devices with their start and end apart: 37, of which 19 were waited for; matrix products, arithmetic and copies ran while one was open for 30% of the time, Pallas kernels for 0%

commit v1 on v0

--- a/solution.py
+++ b/solution.py
@@ -282,7 +282,7 @@
         grad_down_bias,
     )
     small_sizes = [piece.shape[0] for piece in small_grads]
-    small_total = lax.psum(jnp.concatenate(small_grads), ("seq", "batch"))
+    small_total = jnp.sum(lax.all_gather(jnp.concatenate(small_grads), ("seq", "batch")), axis=0)
     summed_small = []
     offset = 0
     for size in small_sizes:

time: 820 us -> 826 us (level)
  waiting for transfers between devices: 246 us -> 320 us
  blocking collectives: 64.8 us -> 0 us
    reduce_scatter x3, waiting for transfers between devices: 0.02 us -> 85.5 us  [batch_gathered_grad(): return lax.psum_scatter(partial, 'seq', scatter_dimension=1, tiled=True)]
    psum x1 -> x0, blocking collectives: 64.8 us -> none  [on_device(): small_total = lax.psum(jnp.concatenate(small_grads), ('seq', 'batch'))]
    ppermute x23, waiting for transfers between devices: 97.9 us -> 71.9 us  [exchange(): got.append(lax.ppermute(piece, axis, pairs))]
    reduce_scatter x2, waiting for transfers between devices: 31.7 us -> 45.5 us  [seq_gathered_grad(): return lax.psum_scatter(partial, 'batch', scatter_dimension=0, tiled=True)]
    unnamed x100 -> x93, local copies, waits for them, and re-layouts: 33.6 us -> 34.2 us
  transfers between devices with their start and end apart: 37 -> 38, of which waited for: 19 -> 20; matrix products, arithmetic and copies ran while one was open for 30% -> 30% of each run, Pallas kernels for 0% -> 0%
where the time goes in v1:
time: 826 us; the launch traced here: 820 us
  waiting for transfers between devices  320 us (39%)
  matrix products  207 us (25%)
  local copies, waits for them, and re-layouts  121 us (15%)
  starting transfers between devices  112 us (14%)
  other arithmetic  45.4 us (5%)
  between operations  15 us (2%)
    ppermute x23, starting transfers between devices, exchange(): got.append(lax.ppermute(piece, axis, pairs))  92 us
    reduce_scatter x3, waiting for transfers between devices, batch_gathered_grad(): return lax.psum_scatter(partial, 'seq', scatter_dimension=1, tiled=True)  85.5 us
    ppermute x23, waiting for transfers between devices, exchange(): got.append(lax.ppermute(piece, axis, pairs))  71.9 us
    reduce_scatter x2, waiting for transfers between devices, seq_gathered_grad(): return lax.psum_scatter(partial, 'batch', scatter_dimension=0, tiled=True)  45.5 us
    all_to_all x1, waiting for transfers between devices, on_device(): lax.all_to_all(packed.reshape(local_rows, 3, seq_count, feature_count //...  41.7 us
    all_to_all x1, waiting for transfers between devices, on_device(): lax.all_to_all(jnp.stack([grad_query, grad_key, grad_value], axis=1)[:, :...  41.1 us
    dot_general x5, matrix products, product(): return jnp.dot(left, right, preferred_element_type=jnp.float32)  40.5 us
    dot_general x5, matrix products, times_transposed(): lax.dot_general(left, right, (((1,), (1,)), ((), ())), preferred_element_...  36.1 us
  transfers between devices with their start and end apart: 38, of which 20 were waited for; matrix products, arithmetic and copies ran while one was open for 30% of the time, Pallas kernels for 0%

profile of v1, /device:TPU:0, one launch (start us, length us, event | category | flops | bytes accessed | tf_op | source)
XLA Modules:
  0.0 820.1 jit_solution(1159621269381390586)
XLA Ops:
  14.6 7.2 convolution_convert_fusion
  28.4 6.8 all-to-all-start
  35.6 41.7 %all-to-all-done = bf16[256,3,8,144]{0,3,1,2:T(8,128)(2,1)} async-done(((bf16[256,3,8,144]{0,3,1,2:T(8,128)(2,1)}), bf16[256,3,8,144]{0,3,1,2:T(8,128)(2,1)}, u32[]{:S(2)}, u32[]{:S(2)}) %all-to-all-start) | async-done | bytes 1769504 | tf_op jit(solution)/shard_map/all_to_all | solution.py:207
  92.6 36.5 %while.27 = (s32[]{:T(128)}, bf16[4,512,144]{1,2,0:T(8,128)(2,1)}, f32[4,2,512,1]{2,1,3,0:T(2,128)S(1)}, s32[4,512]{1,0:T(4,128)S(1)}, s32[2048]{0:T(1024)S(1)},...) while((s32[]{:T(128)}, bf16[4,512,144]{1,2,0:T(8,128)(2,1)}, ...), condition=%wide.region_7.8_spmd, body=%wide.region_4.7_spmd.sunk | while | flops 628169728 | bytes 33537152 | solution.py:74
  140.6 16.1 %all-to-all-done.1 = bf16[8,256,144]{1,2,0:T(8,128)(2,1)} async-done(((bf16[8,256,144]{1,2,0:T(8,128)(2,1)}), bf16[8,256,144]{1,2,0:T(8,128)(2,1)}, u32[]{:S(2)}, u32[]{:S(2)}) %all-to-all-start.1) | async-done | bytes 589856 | tf_op jit(solution)/shard_map/all_to_all | solution.py:219
  161.4 17.2 %multiply_convert_fusion.1 = (bf16[256,4608]{1,0:T(8,128)(2,1)}, f32[256,4608]{1,0:T(8,128)}, f32[256,4608]{1,0:T(8,128)}) fusion(f32[4608]{0:T(1024)S(1)} %convert_element_type.104, bf16[256,1152]{1,0:T(8,128)(2,1)} %add_convert_fusion.2, bf16[1152,4608]{1,0:T(8,128)(2,1)} %param.33), kind=kOutput, calls=%fused_computation.61 | convolution fusion | flops 2795765760 | bytes 23021568 | tf_op jit(solution)/shard_map/dot_general | solution.py:12
  178.6 14.0 %convert_reduce_fusion = (f32[4608]{0:T(1024)S(1)}, bf16[256,4608]{1,0:T(8,128)(2,1)}) fusion(f32[256,4608]{1,0:T(8,128)} %get-tuple-element.309, f32[256,4608]{1,0:T(8,128)} %get-tuple-element.357, bf16[4608,1152]{1,0:T(8,128)(2,1)} %param.35, bf16[1,256,1152]{2,1,0:T(8,128)(2,1)S(1)} %copy-done.13), kind=kOutput, calls=%fused_computation.59 | convolution fusion | flops 2736778752 | bytes 23021568 | tf_op jit(solution)/shard_map/dot_general | solution.py:22
  192.6 8.1 multiply_reduce_fusion.1
  212.7 15.9 %all-to-all-done.2 = bf16[256,8,144]{0,2,1:T(8,128)(2,1)S(1)} async-done(((bf16[256,8,144]{0,2,1:T(8,128)(2,1)}), bf16[256,8,144]{0,2,1:T(8,128)(2,1)S(1)}, u32[]{:S(2)}, u32[]{:S(2)}) %all-to-all-start.2) | async-done | bytes 589856 | tf_op jit(solution)/shard_map/all_to_all | solution.py:245
  231.0 96.8 %while.28 = (s32[]{:T(128)}, f32[2048,2,72]{0,2,1:T(8,128)S(1)}, f32[2048,2,72]{0,2,1:T(8,128)}, bf16[4,512,144]{1,2,0:T(8,128)(2,1)}, bf16[4,512,2,72]{1,3,2,0:...) while((s32[]{:T(128)}, f32[2048,2,72]{0,2,1:T(8,128)S(1)}, ...), condition=%wide.region_14.15_spmd.clone, body=%wide.region_12.14_spmd.clone.sunk | while | flops 1543781376 | bytes 144143088 | solution.py:120
  336.1 8.6 %reshape.487 = bf16[8,2,55296]{2,1,0:T(2,128)(2,1)} reshape(bf16[2048,1,3,144]{3,2,1,0:T(4,128)(2,1)} %bitcast.291) | data formatting | bytes 3538944
  349.2 41.1 %all-to-all-done.3 = bf16[8,2,55296]{2,1,0:T(2,128)(2,1)S(1)} async-done(((bf16[8,2,55296]{2,1,0:T(2,128)(2,1)}), bf16[8,2,55296]{2,1,0:T(2,128)(2,1)S(1)}, u32[]{:S(2)}, u32[]{:S(2)}) %all-to-all-start.3) | async-done | bytes 1769504 | tf_op jit(solution)/shard_map/all_to_all | solution.py:251
  390.4 6.8 reshape.488
  397.2 6.9 copy.151
  404.1 6.6 multiply_reduce_fusion.2
  435.1 5.4 copy.150
  456.7 23.3 %collective-permute-done.5 = bf16[256,432]{0,1:T(8,128)(2,1)S(1)} collective-permute-done((bf16[256,432]{0,1:T(8,128)(2,1)S(1)}, bf16[256,432]{0,1:T(8,128)(2,1)S(1)}, u32[]{:S(2)}, u32[]{:S(2)}) %collective-permute-start.5) | collective-permute-done | bytes 221216 | tf_op jit(solution)/shard_map/ppermute | solution.py:142
  487.1 7.0 fusion.53
  505.6 7.6 collective-permute-done.20
  513.2 6.2 collective-permute-done.21
  525.7 8.0 fusion.48
  547.4 5.4 fusion.60
  556.1 12.8 %collective-permute-start.13 = (bf16[256,576]{0,1:T(8,128)(2,1)S(1)}, bf16[256,576]{0,1:T(8,128)(2,1)S(1)}, u32[]{:S(2)}, u32[]{:S(2)}) collective-permute-start(bf16[256,576]{0,1:T(8,128)(2,1)S(1)} %get-tuple-element.324), channel_id=1, source_target_pairs={{0,4},{4,8},{8,12},{12,16},{16,20},{20,24},{24,28},{28,0},{1,5},{5... | collective-permute-start | bytes 884744 | tf_op jit(solution)/shard_map/ppermute | solution.py:142
  568.8 34.4 %collective-permute-start.14 = (bf16[256,576]{0,1:T(8,128)(2,1)S(1)}, bf16[256,576]{0,1:T(8,128)(2,1)S(1)}, u32[]{:S(2)}, u32[]{:S(2)}) collective-permute-start(bf16[256,576]{0,1:T(8,128)(2,1)S(1)} %get-tuple-element.323), channel_id=1, source_target_pairs={{0,8},{4,12},{8,16},{12,20},{16,24},{20,28},{24,0},{28,4},{1,9},{5... | collective-permute-start | bytes 884744 | tf_op jit(solution)/shard_map/ppermute | solution.py:142
  604.0 11.4 %collective-permute-start.15 = (bf16[256,576]{0,1:T(8,128)(2,1)S(1)}, bf16[256,576]{0,1:T(8,128)(2,1)S(1)}, u32[]{:S(2)}, u32[]{:S(2)}) collective-permute-start(bf16[256,576]{0,1:T(8,128)(2,1)S(1)} %get-tuple-element.322), channel_id=1, source_target_pairs={{0,12},{4,16},{8,20},{12,24},{16,28},{20,0},{24,4},{28,8},{1,13},{... | collective-permute-start | bytes 884744 | tf_op jit(solution)/shard_map/ppermute | solution.py:142
  617.8 7.7 collective-permute-start.18
  635.8 6.6 collective-permute-done.16
  653.7 8.9 %fusion.50 = f32[1152,576]{1,0:T(8,128)} fusion(bf16[2048,1152]{1,0:T(8,128)(2,1)} %all-gather.16.cloned.1.call-done, bf16[2048,576]{0,1:T(8,128)(2,1)} %bitcast.307, pred[2048]{0:T(1024)(128)(4,1)S(1)} %broadcast_in_dim.155), kind=kOutput, calls=%fused_computation.87 | convolution fusion | flops 2719088640 | bytes 9734144 | tf_op jit(solution)/shard_map/dot_general | solution.py:16
  663.9 8.8 %fusion.47 = bf16[1,256,1152]{2,1,0:T(8,128)(2,1)} fusion(f32[256,1152]{1,0:T(8,128)S(1)} %copy-done.8, bf16[256,4608]{1,0:T(8,128)(2,1)} %get-tuple-element.308, bf16[4608,1152]{1,0:T(8,128)(2,1)} %param.35, f32[1152]{0:T(1024)S(1)} %convert_element_type.106), kind=kOutput, calls=%fused_computation.82 | convolution fusion | flops 2718793728 | bytes 14750208 | tf_op jit(solution)/shard_map/dot_general | solution.py:12
  682.4 45.1 %reduce-scatter.14.cloned.1.call-done = f32[1152,144]{0,1:T(8,128)} async-done(((f32[1152,1152]{0,1:T(8,128)}), f32[1152,144]{0,1:T(8,128)}) %reduce-scatter.14.cloned.1.call-update) | async-done | bytes 663568 | tf_op jit(solution)/shard_map/reduce_scatter | solution.py:165
  727.5 40.4 %reduce-scatter.6.cloned.1.call-done = f32[576,144]{0,1:T(8,128)} async-done(((f32[576,1152]{0,1:T(8,128)}), f32[576,144]{0,1:T(8,128)}) %reduce-scatter.6.cloned.1.call-update) | async-done | bytes 331792 | tf_op jit(solution)/shard_map/reduce_scatter | solution.py:165
  767.9 45.4 %reduce-scatter.12.cloned.1.call-done = f32[288,576]{1,0:T(8,128)} async-done(((f32[1152,576]{1,0:T(8,128)}), f32[288,576]{1,0:T(8,128)}) %reduce-scatter.12.cloned.1.call-update) | async-done | bytes 663568 | tf_op jit(solution)/shard_map/reduce_scatter | solution.py:158
  (357 shorter events, 323.1 us)
Async XLA Ops:
  28.4 48.9 %all-to-all-start = ((bf16[256,3,8,144]{0,3,1,2:T(8,128)(2,1)}), bf16[256,3,8,144]{0,3,1,2:T(8,128)(2,1)}, u32[]{:S(2)}, u32[]{:S(2)}) async-start(bf16[256,3,8,144]{0,3,1,2:T(8,128)(2,1)} %copy.125), calls=%async_computation | async-start | bytes 3538944 | tf_op jit(solution)/shard_map/all_to_all | solution.py:207
  135.7 20.9 %all-to-all-start.1 = ((bf16[8,256,144]{1,2,0:T(8,128)(2,1)}), bf16[8,256,144]{1,2,0:T(8,128)(2,1)}, u32[]{:S(2)}, u32[]{:S(2)}) async-start(bf16[8,256,144]{1,2,0:T(8,128)(2,1)} %copy.129), calls=%async_computation.1 | async-start | bytes 1179648 | tf_op jit(solution)/shard_map/all_to_all | solution.py:219
  139.9 290.7 %all-gather.14.cloned.1.call-start = ((), (), s32[]{:S(2)}) async-start(), calls=%async_computation.13 | async-start | bytes 2949120 | tf_op jit(solution)/shard_map/all_gather | solution.py:163
  208.3 20.2 %all-to-all-start.2 = ((bf16[256,8,144]{0,2,1:T(8,128)(2,1)}), bf16[256,8,144]{0,2,1:T(8,128)(2,1)S(1)}, u32[]{:S(2)}, u32[]{:S(2)}) async-start(bf16[256,8,144]{0,2,1:T(8,128)(2,1)} %bitcast.18), calls=%async_computation.2 | async-start | bytes 1179648 | tf_op jit(solution)/shard_map/all_to_all | solution.py:245
  211.9 275.2 %all-gather.12.cloned.1.call-start = ((), (), s32[]{:S(2)}) async-start(), calls=%async_computation.11 | async-start | bytes 5308416 | tf_op jit(solution)/shard_map/all_gather | solution.py:155
  344.6 45.7 %all-to-all-start.3 = ((bf16[8,2,55296]{2,1,0:T(2,128)(2,1)}), bf16[8,2,55296]{2,1,0:T(2,128)(2,1)S(1)}, u32[]{:S(2)}, u32[]{:S(2)}) async-start(bf16[8,2,55296]{2,1,0:T(2,128)(2,1)} %reshape.487), calls=%async_computation.3 | async-start | bytes 3538944 | tf_op jit(solution)/shard_map/all_to_all | solution.py:251
  348.4 177.3 %all-gather.18.cloned.1.call-start = ((), (), s32[]{:S(2)}) async-start(), calls=%async_computation.18 | async-start | bytes 2949120 | tf_op jit(solution)/shard_map/all_gather | solution.py:163
  349.2 198.2 %all-gather.10.cloned.1.call-start = ((), (), s32[]{:S(2)}) async-start(), calls=%async_computation.9 | async-start | bytes 2949120 | tf_op jit(solution)/shard_map/all_gather | solution.py:163
  413.3 240.4 %all-gather.16.cloned.1.call-start = ((), (), s32[]{:S(2)}) async-start(), calls=%async_computation.15 | async-start | bytes 5308416 | tf_op jit(solution)/shard_map/all_gather | solution.py:155
  413.9 264.9 %all-gather.20.cloned.1.call-start = ((), (), s32[]{:S(2)}) async-start(), calls=%async_computation.19 | async-start | bytes 1672704 | tf_op jit(solution)/shard_map/all_gather | solution.py:285
  414.8 267.6 %reduce-scatter.10.cloned.1.call-start = ((), (), s32[]{:S(2)}) async-start(), calls=%async_computation.14 | async-start | bytes 1990656 | tf_op jit(solution)/shard_map/reduce_scatter | solution.py:165
  419.1 10.7 %collective-permute-start.12 = (bf16[256,288]{0,1:T(8,128)(2,1)S(1)}, bf16[256,288]{0,1:T(8,128)(2,1)S(1)}, u32[]{:S(2)}, u32[]{:S(2)}) collective-permute-start(bf16[256,288]{0,1:T(8,128)(2,1)S(1)} %get-tuple-element.342), channel_id=1, source_target_pairs={{0,3},{1,0},{2,1},{3,2},{4,7},{5,4},{6,5},{7,6},{8,11},{9,8},{10,9... | collective-permute-start | bytes 442376 | tf_op jit(solution)/shard_map/ppermute | solution.py:142
  435.1 247.4 %reduce-scatter.8.cloned.1.call-start = ((), (), s32[]{:S(2)}) async-start(), calls=%async_computation.12 | async-start | bytes 2949120 | tf_op jit(solution)/shard_map/reduce_scatter | solution.py:158
  442.6 10.3 %collective-permute-start.4 = (bf16[256,432]{0,1:T(8,128)(2,1)S(1)}, bf16[256,432]{0,1:T(8,128)(2,1)S(1)}, u32[]{:S(2)}, u32[]{:S(2)}) collective-permute-start(bf16[256,432]{0,1:T(8,128)(2,1)S(1)} %get-tuple-element.332), channel_id=1, source_target_pairs={{0,8},{4,12},{8,16},{12,20},{16,24},{20,28},{24,0},{28,4},{1,9},{5... | collective-permute-start | bytes 663560 | tf_op jit(solution)/shard_map/ppermute | solution.py:142
  442.6 37.3 %collective-permute-start.5 = (bf16[256,432]{0,1:T(8,128)(2,1)S(1)}, bf16[256,432]{0,1:T(8,128)(2,1)S(1)}, u32[]{:S(2)}, u32[]{:S(2)}) collective-permute-start(bf16[256,432]{0,1:T(8,128)(2,1)S(1)} %get-tuple-element.331), channel_id=1, source_target_pairs={{0,12},{4,16},{8,20},{12,24},{16,28},{20,0},{24,4},{28,8},{1,13},{... | collective-permute-start | bytes 663560 | tf_op jit(solution)/shard_map/ppermute | solution.py:142
  442.8 37.8 %collective-permute-start.6 = (bf16[256,432]{0,1:T(8,128)(2,1)S(1)}, bf16[256,432]{0,1:T(8,128)(2,1)S(1)}, u32[]{:S(2)}, u32[]{:S(2)}) collective-permute-start(bf16[256,432]{0,1:T(8,128)(2,1)S(1)} %get-tuple-element.330), channel_id=1, source_target_pairs={{0,16},{4,20},{8,24},{12,28},{16,0},{20,4},{24,8},{28,12},{1,17},{... | collective-permute-start | bytes 663560 | tf_op jit(solution)/shard_map/ppermute | solution.py:142
  446.7 34.6 %collective-permute-start.7 = (bf16[256,432]{0,1:T(8,128)(2,1)S(1)}, bf16[256,432]{0,1:T(8,128)(2,1)S(1)}, u32[]{:S(2)}, u32[]{:S(2)}) collective-permute-start(bf16[256,432]{0,1:T(8,128)(2,1)S(1)} %get-tuple-element.329), channel_id=1, source_target_pairs={{0,20},{4,24},{8,28},{12,0},{16,4},{20,8},{24,12},{28,16},{1,21},{... | collective-permute-start | bytes 663560 | tf_op jit(solution)/shard_map/ppermute | solution.py:142
  451.6 30.4 %collective-permute-start.8 = (bf16[256,432]{0,1:T(8,128)(2,1)S(1)}, bf16[256,432]{0,1:T(8,128)(2,1)S(1)}, u32[]{:S(2)}, u32[]{:S(2)}) collective-permute-start(bf16[256,432]{0,1:T(8,128)(2,1)S(1)} %get-tuple-element.328), channel_id=1, source_target_pairs={{0,24},{4,28},{8,0},{12,4},{16,8},{20,12},{24,16},{28,20},{1,25},{... | collective-permute-start | bytes 663560 | tf_op jit(solution)/shard_map/ppermute | solution.py:142
  452.9 29.8 %collective-permute-start.9 = (bf16[256,432]{0,1:T(8,128)(2,1)S(1)}, bf16[256,432]{0,1:T(8,128)(2,1)S(1)}, u32[]{:S(2)}, u32[]{:S(2)}) collective-permute-start(bf16[256,432]{0,1:T(8,128)(2,1)S(1)} %get-tuple-element.327), channel_id=1, source_target_pairs={{0,28},{4,0},{8,4},{12,8},{16,12},{20,16},{24,20},{28,24},{1,29},{... | collective-permute-start | bytes 663560 | tf_op jit(solution)/shard_map/ppermute | solution.py:142
  494.1 233.4 %reduce-scatter.14.cloned.1.call-start = ((), (), s32[]{:S(2)}) async-start(), calls=%async_computation.17 | async-start | bytes 5971968 | tf_op jit(solution)/shard_map/reduce_scatter | solution.py:165
  502.3 10.9 %collective-permute-start.20 = (bf16[256,1152]{1,0:T(8,128)(2,1)S(1)}, bf16[256,1152]{1,0:T(8,128)(2,1)S(1)}, u32[]{:S(2)}, u32[]{:S(2)}) collective-permute-start(bf16[256,1152]{1,0:T(8,128)(2,1)S(1)} %bitcast.317), channel_id=1, source_target_pairs={{0,1},{1,2},{2,3},{3,0},{4,5},{5,6},{6,7},{7,4},{8,9},{9,10},{10,1... | collective-permute-start | bytes 1769480 | tf_op jit(solution)/shard_map/ppermute | solution.py:142
  503.7 15.7 %collective-permute-start.21 = (bf16[256,1152]{1,0:T(8,128)(2,1)S(1)}, bf16[256,1152]{1,0:T(8,128)(2,1)S(1)}, u32[]{:S(2)}, u32[]{:S(2)}) collective-permute-start(bf16[256,1152]{1,0:T(8,128)(2,1)S(1)} %bitcast.318), channel_id=1, source_target_pairs={{0,2},{1,3},{2,0},{3,1},{4,6},{5,7},{6,4},{7,5},{8,10},{9,11},{10,... | collective-permute-start | bytes 1769480 | tf_op jit(solution)/shard_map/ppermute | solution.py:142
  503.9 15.5 %collective-permute-start.22 = (bf16[256,1152]{1,0:T(8,128)(2,1)S(1)}, bf16[256,1152]{1,0:T(8,128)(2,1)S(1)}, u32[]{:S(2)}, u32[]{:S(2)}) collective-permute-start(bf16[256,1152]{1,0:T(8,128)(2,1)S(1)} %bitcast.319), channel_id=1, source_target_pairs={{0,3},{1,0},{2,1},{3,2},{4,7},{5,4},{6,5},{7,6},{8,11},{9,8},{10,9... | collective-permute-start | bytes 1769480 | tf_op jit(solution)/shard_map/ppermute | solution.py:142
  533.7 234.2 %reduce-scatter.6.cloned.1.call-start = ((), (), s32[]{:S(2)}) async-start(), calls=%async_computation.10 | async-start | bytes 3317760 | tf_op jit(solution)/shard_map/reduce_scatter | solution.py:165
  552.8 260.5 %reduce-scatter.12.cloned.1.call-start = ((), (), s32[]{:S(2)}) async-start(), calls=%async_computation.16 | async-start | bytes 3686400 | tf_op jit(solution)/shard_map/reduce_scatter | solution.py:158
  556.1 61.7 %collective-permute-start.13 = (bf16[256,576]{0,1:T(8,128)(2,1)S(1)}, bf16[256,576]{0,1:T(8,128)(2,1)S(1)}, u32[]{:S(2)}, u32[]{:S(2)}) collective-permute-start(bf16[256,576]{0,1:T(8,128)(2,1)S(1)} %get-tuple-element.324), channel_id=1, source_target_pairs={{0,4},{4,8},{8,12},{12,16},{16,20},{20,24},{24,28},{28,0},{1,5},{5... | collective-permute-start | bytes 884744 | tf_op jit(solution)/shard_map/ppermute | solution.py:142
  568.8 57.5 %collective-permute-start.14 = (bf16[256,576]{0,1:T(8,128)(2,1)S(1)}, bf16[256,576]{0,1:T(8,128)(2,1)S(1)}, u32[]{:S(2)}, u32[]{:S(2)}) collective-permute-start(bf16[256,576]{0,1:T(8,128)(2,1)S(1)} %get-tuple-element.323), channel_id=1, source_target_pairs={{0,8},{4,12},{8,16},{12,20},{16,24},{20,28},{24,0},{28,4},{1,9},{5... | collective-permute-start | bytes 884744 | tf_op jit(solution)/shard_map/ppermute | solution.py:142
  604.0 31.1 %collective-permute-start.15 = (bf16[256,576]{0,1:T(8,128)(2,1)S(1)}, bf16[256,576]{0,1:T(8,128)(2,1)S(1)}, u32[]{:S(2)}, u32[]{:S(2)}) collective-permute-start(bf16[256,576]{0,1:T(8,128)(2,1)S(1)} %get-tuple-element.322), channel_id=1, source_target_pairs={{0,12},{4,16},{8,20},{12,24},{16,28},{20,0},{24,4},{28,8},{1,13},{... | collective-permute-start | bytes 884744 | tf_op jit(solution)/shard_map/ppermute | solution.py:142
  615.4 27.0 %collective-permute-start.16 = (bf16[256,576]{0,1:T(8,128)(2,1)S(1)}, bf16[256,576]{0,1:T(8,128)(2,1)S(1)}, u32[]{:S(2)}, u32[]{:S(2)}) collective-permute-start(bf16[256,576]{0,1:T(8,128)(2,1)S(1)} %get-tuple-element.321), channel_id=1, source_target_pairs={{0,16},{4,20},{8,24},{12,28},{16,0},{20,4},{24,8},{28,12},{1,17},{... | collective-permute-start | bytes 884744 | tf_op jit(solution)/shard_map/ppermute | solution.py:142
  615.4 27.7 %collective-permute-start.17 = (bf16[256,576]{0,1:T(8,128)(2,1)S(1)}, bf16[256,576]{0,1:T(8,128)(2,1)S(1)}, u32[]{:S(2)}, u32[]{:S(2)}) collective-permute-start(bf16[256,576]{0,1:T(8,128)(2,1)S(1)} %get-tuple-element.320), channel_id=1, source_target_pairs={{0,20},{4,24},{8,28},{12,0},{16,4},{20,8},{24,12},{28,16},{1,21},{... | collective-permute-start | bytes 884744 | tf_op jit(solution)/shard_map/ppermute | solution.py:142
  617.8 26.1 %collective-permute-start.18 = (bf16[256,576]{0,1:T(8,128)(2,1)S(1)}, bf16[256,576]{0,1:T(8,128)(2,1)S(1)}, u32[]{:S(2)}, u32[]{:S(2)}) collective-permute-start(bf16[256,576]{0,1:T(8,128)(2,1)S(1)} %get-tuple-element.319), channel_id=1, source_target_pairs={{0,24},{4,28},{8,0},{12,4},{16,8},{20,12},{24,16},{28,20},{1,25},{... | collective-permute-start | bytes 884744 | tf_op jit(solution)/shard_map/ppermute | solution.py:142
  626.3 22.6 %collective-permute-start.19 = (bf16[256,576]{0,1:T(8,128)(2,1)S(1)}, bf16[256,576]{0,1:T(8,128)(2,1)S(1)}, u32[]{:S(2)}, u32[]{:S(2)}) collective-permute-start(bf16[256,576]{0,1:T(8,128)(2,1)S(1)} %get-tuple-element.318), channel_id=1, source_target_pairs={{0,28},{4,0},{8,4},{12,8},{16,12},{20,16},{24,20},{28,24},{1,29},{... | collective-permute-start | bytes 884744 | tf_op jit(solution)/shard_map/ppermute | solution.py:142
  (53 other events, 575.2 us)
Sparse Core Ops, SparseCore 0:
  203.4 36.2 all-gather.13
  241.3 51.1 all-gather.11
  351.1 38.6 all-gather.17
  413.4 37.5 all-gather.9
  452.6 72.2 all-gather.15
  527.6 55.9 all-gather.19
  586.5 36.7 reduce-scatter.9
  626.9 37.2 reduce-scatter.7
  667.0 60.4 reduce-scatter.13
  730.3 37.6 reduce-scatter.5
  771.6 41.7 reduce-scatter.11
